TPU v7x, 32 devices: a whole 2x2x4 slice. The times are simulated.
32 devices in a mesh: row: 4 (over y, core), col: 8 (over z, x).
Axes of the slice: x: 2, y: 2, z: 4, core: 2. Of those that a mesh axis runs over, the one named last changes fastest.
Arguments:
- adjacency: int32 [8192, 8192], P('row', 'col'), may hold values from 0 to 1, as said below
Outputs:
- closure: bfloat16 [8192, 8192], P('row', 'col')
Inputs may be any that keep to these rules, and one draw needn't show every extreme that they name: `adjacency`: every entry is 0 or 1; there is no bound on the number of ones in a row, a column or a block, and their share differs widely between rows and between columns.
All inputs are finite; a program needn't handle non-finite values.
Results may differ from a plain program's by a relative error of at most 0.001.
Values may be sent and summed in bfloat16 or wider, within the bound.
A program may use at most 192 MiB of HBM per device.

v0:
```python
import functools

import jax
import jax.numpy as jnp
from jax import lax
from jax.experimental import pallas as pl
from jax.experimental.pallas import tpu as pltpu
from jax.sharding import PartitionSpec as P

PANEL = 512
PANELS = 4

CHUNK = 8
CONVERT = 16
EVERY = CONVERT // CHUNK
FREE = 8
RIGHT = 128
LOAD = 128
FIRST = 128
GROUP = 256
TAIL = 128
SPLIT = 32
TILE = 512
UNIT = 256
RING = 32
CREDIT = 16
EARLY = ({1: 4}, {})
LATE = ({1: 4, 3: 4}, {})
PACE = RIGHT // (2 * CHUNK)
MESH = pl.DeviceIdType.MESH


def lag_of(row):
    return PACE * (1 + row) + (3 * PACE // 2) * (row // 2)


def kernel(n_rows, n_cols, window, adj_hbm, out, left, right, partial, adj,
           adj_sem, z_send, b_send, z_recv, x_send, x_recv, r_send, r_recv, credit, f_send, ready):
    block_rows, block_cols = adj.shape
    holders = left.shape[0]
    stages = n_cols // holders
    n_chunks = block_rows // CHUNK
    n_right = window // RIGHT
    n_units = block_cols // UNIT
    tail_from = n_chunks - TAIL // CHUNK
    split_from = n_chunks - SPLIT // CHUNK
    early, late = ([{stage: chunks for stage, chunks in core.items() if stage < n_cols // holders} for core in spare]
                   for spare in (EARLY, LATE))
    spared_by = [sorted({*a, *b}) for a, b in zip(early, late)]
    cores = [core for core in range(2) if spared_by[core]]

    r = lax.axis_index("row")
    c = lax.axis_index("col")
    hi = c // holders
    lo = lax.rem(c, holders)
    lag = lag_of(r)

    relay = lax.rem(hi, 2) == 0
    feeds_next = relay & (hi < stages - 1)
    feeds_back = relay & (hi > 0)
    next_col = c + holders * (1 + (hi + 2 < stages).astype(jnp.int32))
    back_col = c - holders

    source = jnp.where(relay, c - 2 * holders, jnp.where(hi == stages - 1, back_col, c + holders))
    as_next = relay | (hi == stages - 1)
    on_core = [lax.rem(r, 2) == core for core in range(2)]
    spared = [jnp.int32(0)] * 2
    for i, spare in enumerate((early, late)):
        for core in cores:
            for stage, chunks in spare[core].items():
                spared[i] = jnp.where(on_core[core] & (hi == stage), chunks, spared[i])

    def crosses(j):
        return (j < split_from - spared[0]) | ((j >= split_from) & (j < n_chunks - spared[1]))

    def load(start, size, sem):
        rows = pl.ds(pl.multiple_of(start, CONVERT), size)
        return pltpu.make_async_copy(adj_hbm.at[rows], adj.at[rows], adj_sem.at[sem])

    head = load(0, FIRST, 0)
    rest = load(FIRST, block_rows - FIRST, 1)

    def chunk(j):
        return pl.ds(pl.multiple_of(j * CHUNK, CHUNK), CHUNK)

    def z_copy(j):
        part = left.at[lo, chunk(j)]
        return pltpu.make_async_remote_copy(
            src_ref=part, dst_ref=part, send_sem=z_send, recv_sem=z_recv.at[lax.rem(j, RING)],
            device_id={"col": next_col}, device_id_type=MESH)

    def z_back(j):
        part = left.at[lo, chunk(j)]
        return pltpu.make_async_remote_copy(
            src_ref=part, dst_ref=part, send_sem=b_send, recv_sem=z_recv.at[lax.rem(j, RING)],
            device_id={"col": back_col}, device_id_type=MESH)

    def x_group(j):
        return j // (GROUP // CHUNK) + (j >= tail_from).astype(jnp.int32) + (j >= split_from).astype(jnp.int32)

    def x_copy(d, j):
        part = left.at[lo, chunk(j)]
        peer = hi * holders + lax.rem(lo + d, holders)
        return pltpu.make_async_remote_copy(
            src_ref=part, dst_ref=part, send_sem=x_send.at[d - 1], recv_sem=x_recv.at[d - 1, x_group(j)],
            device_id={"col": peer}, device_id_type=MESH)

    def x_arrival(d, group, start, size):
        part = left.at[lax.rem(lo + holders - d, holders), pl.ds(pl.multiple_of(start, CHUNK), size)]
        peer = hi * holders + lax.rem(lo + holders - d, holders)
        return pltpu.make_async_remote_copy(
            src_ref=part, dst_ref=part, send_sem=x_send.at[d - 1], recv_sem=x_recv.at[d - 1, group],
            device_id={"col": peer}, device_id_type=MESH)

    def far_copy(d, stage, chunks, end, sem):
        rows = chunks * CHUNK
        part = left.at[lax.rem(lo + holders - d, holders), pl.ds(end - rows, rows)]
        return pltpu.make_async_remote_copy(
            src_ref=part, dst_ref=part, send_sem=f_send.at[d - 1, sem],
            recv_sem=x_recv.at[d - 1, block_rows // GROUP + (end == block_rows)],
            device_id={"col": stage * holders + lo}, device_id_type=MESH)

    def far_copies(core, spare, end):
        first_sem = len(early[core]) if end == block_rows else 0
        return [far_copy(d, stage, spare[core][stage], end, first_sem + i)
                for i, stage in enumerate(sorted(spare[core], reverse=True)) for d in range(1, holders)]

    def r_rows(i):
        return pl.ds(pl.multiple_of(i * RIGHT, RIGHT), RIGHT)

    def r_copy(i):
        part = right.at[r_rows(i)]
        return pltpu.make_async_remote_copy(
            src_ref=part, dst_ref=part, send_sem=r_send, recv_sem=r_recv.at[i],
            device_id={"row": r + 1}, device_id_type=MESH)

    head.start()

    barrier = pltpu.get_barrier_semaphore()

    def greet(where):
        pl.semaphore_signal(barrier, inc=1, device_id=where, device_id_type=MESH)

    @pl.when(feeds_back)
    def _():
        greet({"col": c - 2 * holders})
        greet({"col": back_col})

    @pl.when(feeds_next)
    def _():
        greet({"col": next_col})

    @pl.when(~relay & (hi < stages - 1))
    def _():
        greet({"col": c + holders})

    @pl.when(~relay & (hi == stages - 1))
    def _():
        greet({"col": c - holders})

    for d in range(1, holders):
        greet({"col": hi * holders + lax.rem(lo + d, holders)})

    for core in cores:
        @pl.when(on_core[core] & (hi == 0))
        def _():
            for stage in spared_by[core]:
                greet({"col": stage * holders + lo})

    @pl.when(r > 0)
    def _():
        greet({"row": r - 1})

    @pl.when(r < n_rows - 1)
    def _():
        greet({"row": r + 1})

    def convert_left(i):
        rows = pl.ds(pl.multiple_of(i * CONVERT, CONVERT), CONVERT)
        left[lo, rows, :] = adj[rows, :].astype(jnp.bfloat16)

    def convert_right(i):
        right[r_rows(i), :] = adj[r_rows(i), :].astype(jnp.bfloat16)

    ahead = FIRST // CONVERT
    behind = ahead // 2

    @pl.loop(FIRST // LOAD, block_rows // LOAD)
    def _(i):
        load(i * LOAD, LOAD, 1).start()

    head.wait()

    @pl.when(hi == 0)
    def _():
        for k in range(ahead):
            convert_left(k)

    known = (2 * feeds_back.astype(jnp.int32) + feeds_next.astype(jnp.int32)
             + (~relay).astype(jnp.int32) + (holders - 1)
             + (r > 0).astype(jnp.int32) + (r < n_rows - 1).astype(jnp.int32))
    spared_here = [on_core[core] & (hi == stage) for core in cores for stage in spared_by[core]]
    for here in spared_here:
        known += here.astype(jnp.int32)
    pl.semaphore_wait(barrier, known)

    for here in spared_here:
        @pl.when(here)
        def _():
            pl.semaphore_signal(ready, inc=1, device_id={"col": lo}, device_id_type=MESH)

    def paid(j):
        return (lax.rem(j, CREDIT) == 0) & (j >= RING)

    def pass_right(j):
        late = j - lag
        i = late // PACE

        @pl.when((late >= 0) & (lax.rem(late, PACE) == 0) & (i < n_right))
        def _():
            @pl.when(r > 0)
            def _():
                r_copy(i).wait_recv()

            @pl.when(r < n_rows - 1)
            def _():
                r_copy(i).start()

    def step(j):
        @pl.when(hi > 0)
        def _():
            z_copy(j).wait_recv()

            @pl.when((lax.rem(j + 1, CREDIT) == 0) & (j + 1 <= n_chunks - RING))
            def _():
                pl.semaphore_signal(credit.at[jnp.where(as_next, 0, 1)], inc=1,
                                    device_id={"col": source}, device_id_type=MESH)

        @pl.when(feeds_next)
        def _():
            @pl.when(paid(j))
            def _():
                pl.semaphore_wait(credit.at[0], 1)

            z_copy(j).start()

        @pl.when(feeds_back)
        def _():
            @pl.when(paid(j))
            def _():
                pl.semaphore_wait(credit.at[1], 1)

            z_back(j).start()

        @pl.when(crosses(j))
        def _():
            for d in range(1, holders):
                x_copy(d, j).start()

        pass_right(j)

        @pl.when(j == EVERY * behind)
        def _():
            rest.wait()

        unit = j // EVERY + ahead - behind

        @pl.when((hi == 0) & (lax.rem(j, EVERY) == 0) & (unit >= ahead) & (unit < block_rows // CONVERT))
        def _():
            convert_left(unit)

        @pl.when((r == 0) & (lax.rem(j, PACE) == 0) & (j < PACE * n_right))
        def _():
            convert_right(j // PACE)

    def compute(u):
        g = u // n_units
        t = lax.rem(u, n_units)

        @pl.when(t == 0)
        def _():
            for d in range(1, holders):
                x_arrival(d, g, g * GROUP, GROUP).wait_recv()

        rows = pl.ds(pl.multiple_of(g * GROUP, GROUP), GROUP)
        cols = pl.ds(pl.multiple_of(t * UNIT, UNIT), UNIT)
        counts = jnp.zeros((GROUP, UNIT), jnp.float32)
        for h in range(holders):
            counts += jnp.dot(left[h, rows, :], right[h * block_cols:(h + 1) * block_cols, cols],
                              preferred_element_type=jnp.float32)
        out[rows, cols] = jnp.where(counts > 0.5, 1, adj[rows, cols]).astype(out.dtype)

    body_units = (block_rows // GROUP - 1) * n_units
    primed = PACE * (n_right - 1) + lag_of(n_rows - 1)
    gap = max(1, (n_chunks - FREE - primed) // body_units)
    first = min(n_chunks, max(primed, n_chunks - FREE - gap * body_units))
    done = min(body_units, (n_chunks - first) // gap)

    @pl.loop(0, first)
    def _(j):
        step(j)

    @pl.loop(first, n_chunks)
    def _(j):
        step(j)

        u = (j - first) // gap

        @pl.when((lax.rem(j - first, gap) == gap - 1) & (u < done))
        def _():
            compute(u)

    @pl.loop(n_chunks, max(n_chunks, primed + 1))
    def _(j):
        pass_right(j)

    @pl.loop(done, body_units)
    def _(u):
        compute(u)

    def arrived(group, start, size):
        for d in range(1, holders):
            x_arrival(d, group, start, size).wait_recv()

    def half(h, start, cols):
        rights = pl.ds(pl.multiple_of(h * block_cols, block_cols), block_cols)
        return jnp.dot(left[h, start:start + TAIL, :], right[rights, cols], preferred_element_type=jnp.float32)

    tiles = [slice(t, t + TILE) for t in range(0, block_cols, TILE)]
    start = block_rows - GROUP
    arrived(block_rows // GROUP - 1, start, TAIL)
    for cols in tiles:
        counts = half(0, start, cols)
        for h in range(1, holders):
            counts += half(h, start, cols)
        out[start:start + TAIL, cols] = jnp.where(
            counts > 0.5, 1, adj[start:start + TAIL, cols]).astype(out.dtype)

    start = block_rows - TAIL
    for cols in tiles:
        partial[:, cols] = half(lo, start, cols) + adj[start:start + TAIL, cols].astype(jnp.float32)

    arrived(block_rows // GROUP, start, TAIL - SPLIT)
    for core in cores:
        @pl.when(on_core[core] & (hi == 0))
        def _():
            pl.semaphore_wait(ready, len(spared_by[core]))
            for copy in far_copies(core, early, block_rows - SPLIT):
                copy.start()

    arrived(block_rows // GROUP + 1, block_rows - SPLIT, SPLIT)
    for core in cores:
        @pl.when(on_core[core] & (hi == 0))
        def _():
            for copy in far_copies(core, late, block_rows):
                copy.start()

    whole = left.at[lo]

    @pl.when(feeds_next)
    def _():
        pltpu.make_async_remote_copy(
            src_ref=whole, dst_ref=whole, send_sem=z_send, recv_sem=z_recv.at[0],
            device_id={"col": next_col}, device_id_type=MESH).wait_send()

    @pl.when(feeds_back)
    def _():
        pltpu.make_async_remote_copy(
            src_ref=whole, dst_ref=whole, send_sem=b_send, recv_sem=z_recv.at[0],
            device_id={"col": back_col}, device_id_type=MESH).wait_send()

    def x_sent(chunks):
        part = left.at[lo, pl.ds(0, chunks * CHUNK)]
        for d in range(1, holders):
            pltpu.make_async_remote_copy(
                src_ref=part, dst_ref=part, send_sem=x_send.at[d - 1], recv_sem=x_recv.at[d - 1, 0],
                device_id={"col": hi * holders + lax.rem(lo + d, holders)}, device_id_type=MESH).wait_send()

    for chunks in sorted({0, *(early[core].get(stage, 0) + late[core].get(stage, 0) for core in cores for stage in spared_by[core])}):
        @pl.when(spared[0] + spared[1] == chunks)
        def _():
            x_sent(n_chunks - chunks)

    for core in cores:
        @pl.when(on_core[core] & (hi == 0))
        def _():
            for copy in far_copies(core, early, block_rows - SPLIT) + far_copies(core, late, block_rows):
                copy.wait_send()

    @pl.when(r < n_rows - 1)
    def _():
        pltpu.make_async_remote_copy(
            src_ref=right, dst_ref=right, send_sem=r_send, recv_sem=r_recv.at[0],
            device_id={"row": r + 1}, device_id_type=MESH).wait_send()


def finish(closed, left, right, partial, out, tail, sems):
    holders = left.shape[0]
    block_rows, block_cols = closed.shape
    lo = lax.rem(lax.axis_index("col"), holders)
    body = block_rows - TAIL
    bulk = pltpu.make_async_copy(closed.at[0:body], out.at[0:body], sems.at[0])
    bulk.start()
    for t in range(0, block_cols, TILE):
        cols = slice(t, t + TILE)
        counts = partial[:, cols]
        for d in range(1, holders):
            h = lax.rem(lo + holders - d, holders)
            rights = pl.ds(pl.multiple_of(h * block_cols, block_cols), block_cols)
            counts += jnp.dot(left[h, body:block_rows, :], right[rights, cols], preferred_element_type=jnp.float32)
        tail[:, cols] = jnp.where(counts > 0.5, 1, 0).astype(tail.dtype)
    last = pltpu.make_async_copy(tail, out.at[body:block_rows], sems.at[1])
    last.start()
    bulk.wait()
    last.wait()


def per_device(n_rows, n_cols, adjacency):
    block_rows, block_cols = adjacency.shape
    window = PANELS * PANEL
    holders = window // block_cols
    dma = pltpu.SemaphoreType.DMA
    parts = pl.pallas_call(
        functools.partial(kernel, n_rows, n_cols, window),
        out_shape=[
            pltpu.VMEM((block_rows, block_cols), jnp.bfloat16),
            pltpu.VMEM((holders, block_rows, block_cols), jnp.bfloat16),
            pltpu.VMEM((window, block_cols), jnp.bfloat16),
            pltpu.VMEM((TAIL, block_cols), jnp.float32),
        ],
        in_specs=[pl.BlockSpec(memory_space=pltpu.HBM)],
        out_specs=[pl.BlockSpec(memory_space=pltpu.VMEM)] * 4,
        scratch_shapes=[
            pltpu.VMEM((block_rows, block_cols), jnp.int32),
            dma((2,)),
            dma,
            dma,
            dma((RING,)),
            dma((holders - 1,)),
            dma((holders - 1, block_rows // GROUP + 2)),
            dma,
            dma((window // RIGHT,)),
            pltpu.SemaphoreType.REGULAR((2,)),
            dma((holders - 1, max(len(a) + len(b) for a, b in zip(EARLY, LATE)))),
            pltpu.SemaphoreType.REGULAR,
        ],
        compiler_params=pltpu.CompilerParams(
            collective_id=0, has_side_effects=True, vmem_limit_bytes=20 * 1024 * 1024),
    )(pltpu.with_memory_space_constraint(adjacency, pltpu.HBM))
    return pl.pallas_call(
        finish,
        out_shape=jax.ShapeDtypeStruct((block_rows, block_cols), jnp.bfloat16),
        in_specs=[pl.BlockSpec(memory_space=pltpu.VMEM)] * 4,
        out_specs=pl.BlockSpec(memory_space=pltpu.HBM),
        scratch_shapes=[pltpu.VMEM((TAIL, block_cols), jnp.bfloat16), dma((2,))],
        compiler_params=pltpu.CompilerParams(vmem_limit_bytes=8 * 1024 * 1024),
    )(*parts)


def solution(mesh):
    spec = P("row", "col")
    return jax.shard_map(
        functools.partial(per_device, mesh.shape["row"], mesh.shape["col"]),
        mesh=mesh, in_specs=(spec,), out_specs=spec, check_vma=False)
```

profile of v0, /device:TPU:12, one launch (start us, length us, event | category | flops | bytes accessed | tf_op | source)
XLA Modules:
  0.0 101.2 jit_solution(2553203611045502067)
XLA Ops:
  0.0 99.2 %shard_map.17 = (bf16[2048,1024]{1,0:T(8,128)(2,1)S(1)}, bf16[2,2048,1024]{2,1,0:T(8,128)(2,1)S(1)}, bf16[2048,1024]{1,0:T(8,128)(2,1)S(1)}, f32[128,1024]{1,0:T(8,128)S(1)}) custom-call(s32[2048,1024]{1,0:T(8,128)} %adj_hbm.1), custom_call_target="tpu_custom_call" | custom-call | tf_op jit(solution)/shard_map/pallas_call | solution.py:423
  99.2 2.0 %shard_map.18 = bf16[2048,1024]{1,0:T(8,128)(2,1)} custom-call(bf16[2048,1024]{1,0:T(8,128)(2,1)S(1)} %get-tuple-element.9.closed, bf16[2,2048,1024]{2,1,0:T(8,128)(2,1)S(1)} %get-tuple-element.10.left, bf16[2048,1024]{1,0:T(8,128)(2,1)S(1)} %get-tuple-element.11.right, f32[128,1024]{1,0:T(8,128)S(1)} %get-tuple-element.12.partial), custom_call_target="tpu_custom_call" | custom-call | tf_op jit(solution)/shard_map/pallas_call | solution.py:450
where the time goes:
time: 101 us
  Pallas kernels  101 us (100%)
    pallas_call x1, Pallas kernels, per_device(): pl.pallas_call(functools.partial(kernel, n_rows, n_cols, window), out_sha...  99.2 us
    pallas_call x1, Pallas kernels, per_device(): pl.pallas_call(finish, out_shape=jax.ShapeDtypeStruct((block_rows, block_...  2.03 us

commit v1 on v0

--- a/solution.py
+++ b/solution.py
@@ -24,8 +24,9 @@
 UNIT = 256
 RING = 32
 CREDIT = 16
-EARLY = ({1: 4}, {})
-LATE = ({1: 4, 3: 4}, {})
+RIGHTS = 4
+EARLY = ({1: 5}, {})
+LATE = ({1: 4, 3: 4}, {1: 2})
 PACE = RIGHT // (2 * CHUNK)
 MESH = pl.DeviceIdType.MESH
 
@@ -131,7 +132,7 @@
     def r_copy(i):
         part = right.at[r_rows(i)]
         return pltpu.make_async_remote_copy(
-            src_ref=part, dst_ref=part, send_sem=r_send, recv_sem=r_recv.at[i],
+            src_ref=part, dst_ref=part, send_sem=r_send, recv_sem=r_recv.at[lax.rem(i, RIGHTS)],
             device_id={"row": r + 1}, device_id_type=MESH)
 
     head.start()
@@ -222,19 +223,22 @@
             def _():
                 r_copy(i).wait_recv()
 
+                @pl.when(i < n_right - RIGHTS)
+                def _():
+                    pl.semaphore_signal(credit.at[2], inc=1, device_id={"row": r - 1}, device_id_type=MESH)
+
             @pl.when(r < n_rows - 1)
             def _():
+                @pl.when(i >= RIGHTS)
+                def _():
+                    pl.semaphore_wait(credit.at[2], 1)
+
                 r_copy(i).start()
 
     def step(j):
         @pl.when(hi > 0)
         def _():
             z_copy(j).wait_recv()
-
-            @pl.when((lax.rem(j + 1, CREDIT) == 0) & (j + 1 <= n_chunks - RING))
-            def _():
-                pl.semaphore_signal(credit.at[jnp.where(as_next, 0, 1)], inc=1,
-                                    device_id={"col": source}, device_id_type=MESH)
 
         @pl.when(feeds_next)
         def _():
@@ -256,6 +260,11 @@
         def _():
             for d in range(1, holders):
                 x_copy(d, j).start()
+
+        @pl.when((hi > 0) & (lax.rem(j + 1, CREDIT) == 0) & (j + 1 <= n_chunks - RING))
+        def _():
+            pl.semaphore_signal(credit.at[jnp.where(as_next, 0, 1)], inc=1,
+                                device_id={"col": source}, device_id_type=MESH)
 
         pass_right(j)
 
@@ -439,8 +448,8 @@
             dma((holders - 1,)),
             dma((holders - 1, block_rows // GROUP + 2)),
             dma,
-            dma((window // RIGHT,)),
-            pltpu.SemaphoreType.REGULAR((2,)),
+            dma((RIGHTS,)),
+            pltpu.SemaphoreType.REGULAR((3,)),
             dma((holders - 1, max(len(a) + len(b) for a, b in zip(EARLY, LATE)))),
             pltpu.SemaphoreType.REGULAR,
         ],

time: 101 us -> 101 us (level)
  no operation moved by 1% of the time
where the time goes in v1:
time: 101 us
  Pallas kernels  101 us (100%)
    pallas_call x1, Pallas kernels, per_device(): pl.pallas_call(functools.partial(kernel, n_rows, n_cols, window), out_sha...  98.6 us
    pallas_call x1, Pallas kernels, per_device(): pl.pallas_call(finish, out_shape=jax.ShapeDtypeStruct((block_rows, block_...  2.03 us

profile of v1, /device:TPU:12, one launch (start us, length us, event | category | flops | bytes accessed | tf_op | source)
XLA Modules:
  0.0 100.6 jit_solution(11580007345786624173)
XLA Ops:
  0.0 98.6 %shard_map.17 = (bf16[2048,1024]{1,0:T(8,128)(2,1)S(1)}, bf16[2,2048,1024]{2,1,0:T(8,128)(2,1)S(1)}, bf16[2048,1024]{1,0:T(8,128)(2,1)S(1)}, f32[128,1024]{1,0:T(8,128)S(1)}) custom-call(s32[2048,1024]{1,0:T(8,128)} %adj_hbm.1), custom_call_target="tpu_custom_call" | custom-call | tf_op jit(solution)/shard_map/pallas_call | solution.py:432
  98.6 2.0 %shard_map.18 = bf16[2048,1024]{1,0:T(8,128)(2,1)} custom-call(bf16[2048,1024]{1,0:T(8,128)(2,1)S(1)} %get-tuple-element.9.closed, bf16[2,2048,1024]{2,1,0:T(8,128)(2,1)S(1)} %get-tuple-element.10.left, bf16[2048,1024]{1,0:T(8,128)(2,1)S(1)} %get-tuple-element.11.right, f32[128,1024]{1,0:T(8,128)S(1)} %get-tuple-element.12.partial), custom_call_target="tpu_custom_call" | custom-call | tf_op jit(solution)/shard_map/pallas_call | solution.py:459

commit v2 on v1

--- a/solution.py
+++ b/solution.py
@@ -18,6 +18,7 @@
 LOAD = 128
 FIRST = 128
 GROUP = 256
+PAIR = 2 * GROUP // CHUNK
 TAIL = 128
 SPLIT = 32
 TILE = 512
@@ -45,6 +46,8 @@
     n_units = block_cols // UNIT
     tail_from = n_chunks - TAIL // CHUNK
     split_from = n_chunks - SPLIT // CHUNK
+    paired = (block_rows // GROUP - 1) // 2
+    tail_sem = block_rows // GROUP - paired - 1
     early, late = ([{stage: chunks for stage, chunks in core.items() if stage < n_cols // holders} for core in spare]
                    for spare in (EARLY, LATE))
     spared_by = [sorted({*a, *b}) for a, b in zip(early, late)]
@@ -97,7 +100,7 @@
             device_id={"col": back_col}, device_id_type=MESH)
 
     def x_group(j):
-        return j // (GROUP // CHUNK) + (j >= tail_from).astype(jnp.int32) + (j >= split_from).astype(jnp.int32)
+        return jnp.minimum(j // PAIR, paired) + jnp.maximum(j // (GROUP // CHUNK) - 2 * paired, 0) + (j >= tail_from).astype(jnp.int32) + (j >= split_from).astype(jnp.int32)
 
     def x_copy(d, j):
         part = left.at[lo, chunk(j)]
@@ -118,7 +121,7 @@
         part = left.at[lax.rem(lo + holders - d, holders), pl.ds(end - rows, rows)]
         return pltpu.make_async_remote_copy(
             src_ref=part, dst_ref=part, send_sem=f_send.at[d - 1, sem],
-            recv_sem=x_recv.at[d - 1, block_rows // GROUP + (end == block_rows)],
+            recv_sem=x_recv.at[d - 1, tail_sem + 1 + (end == block_rows)],
             device_id={"col": stage * holders + lo}, device_id_type=MESH)
 
     def far_copies(core, spare, end):
@@ -286,10 +289,15 @@
         g = u // n_units
         t = lax.rem(u, n_units)
 
-        @pl.when(t == 0)
+        @pl.when((t == 0) & (lax.rem(g, 2) == 0) & (g < 2 * paired))
         def _():
             for d in range(1, holders):
-                x_arrival(d, g, g * GROUP, GROUP).wait_recv()
+                x_arrival(d, g // 2, g * GROUP, 2 * GROUP).wait_recv()
+
+        @pl.when((t == 0) & (g >= 2 * paired))
+        def _():
+            for d in range(1, holders):
+                x_arrival(d, g - paired, g * GROUP, GROUP).wait_recv()
 
         rows = pl.ds(pl.multiple_of(g * GROUP, GROUP), GROUP)
         cols = pl.ds(pl.multiple_of(t * UNIT, UNIT), UNIT)
@@ -337,7 +345,7 @@
 
     tiles = [slice(t, t + TILE) for t in range(0, block_cols, TILE)]
     start = block_rows - GROUP
-    arrived(block_rows // GROUP - 1, start, TAIL)
+    arrived(tail_sem, start, TAIL)
     for cols in tiles:
         counts = half(0, start, cols)
         for h in range(1, holders):
@@ -349,7 +357,7 @@
     for cols in tiles:
         partial[:, cols] = half(lo, start, cols) + adj[start:start + TAIL, cols].astype(jnp.float32)
 
-    arrived(block_rows // GROUP, start, TAIL - SPLIT)
+    arrived(tail_sem + 1, start, TAIL - SPLIT)
     for core in cores:
         @pl.when(on_core[core] & (hi == 0))
         def _():
@@ -357,7 +365,7 @@
             for copy in far_copies(core, early, block_rows - SPLIT):
                 copy.start()
 
-    arrived(block_rows // GROUP + 1, block_rows - SPLIT, SPLIT)
+    arrived(tail_sem + 2, block_rows - SPLIT, SPLIT)
     for core in cores:
         @pl.when(on_core[core] & (hi == 0))
         def _():
@@ -446,7 +454,7 @@
             dma,
             dma((RING,)),
             dma((holders - 1,)),
-            dma((holders - 1, block_rows // GROUP + 2)),
+            dma((holders - 1, block_rows // GROUP + 2 - (block_rows // GROUP - 1) // 2)),
             dma,
             dma((RIGHTS,)),
             pltpu.SemaphoreType.REGULAR((3,)),

time: 101 us -> 101 us (level)
  no operation moved by 1% of the time
where the time goes in v2:
time: 101 us
  Pallas kernels  101 us (100%)
    pallas_call x1, Pallas kernels, per_device(): pl.pallas_call(functools.partial(kernel, n_rows, n_cols, window), out_sha...  98.5 us
    pallas_call x1, Pallas kernels, per_device(): pl.pallas_call(finish, out_shape=jax.ShapeDtypeStruct((block_rows, block_...  2.03 us

profile of v2, /device:TPU:12, one launch (start us, length us, event | category | flops | bytes accessed | tf_op | source)
XLA Modules:
  0.0 100.6 jit_solution(2032496803456886439)
XLA Ops:
  0.0 98.5 %shard_map.17 = (bf16[2048,1024]{1,0:T(8,128)(2,1)S(1)}, bf16[2,2048,1024]{2,1,0:T(8,128)(2,1)S(1)}, bf16[2048,1024]{1,0:T(8,128)(2,1)S(1)}, f32[128,1024]{1,0:T(8,128)S(1)}) custom-call(s32[2048,1024]{1,0:T(8,128)} %adj_hbm.1), custom_call_target="tpu_custom_call" | custom-call | tf_op jit(solution)/shard_map/pallas_call | solution.py:440
  98.5 2.0 %shard_map.18 = bf16[2048,1024]{1,0:T(8,128)(2,1)} custom-call(bf16[2048,1024]{1,0:T(8,128)(2,1)S(1)} %get-tuple-element.9.closed, bf16[2,2048,1024]{2,1,0:T(8,128)(2,1)S(1)} %get-tuple-element.10.left, bf16[2048,1024]{1,0:T(8,128)(2,1)S(1)} %get-tuple-element.11.right, f32[128,1024]{1,0:T(8,128)S(1)} %get-tuple-element.12.partial), custom_call_target="tpu_custom_call" | custom-call | tf_op jit(solution)/shard_map/pallas_call | solution.py:467

commit v3 on v1

--- a/solution.py
+++ b/solution.py
@@ -10,10 +10,10 @@
 PANEL = 512
 PANELS = 4
 
-CHUNK = 8
+CHUNK = 16
 CONVERT = 16
 EVERY = CONVERT // CHUNK
-FREE = 8
+FREE = 4
 RIGHT = 128
 LOAD = 128
 FIRST = 128
@@ -22,11 +22,11 @@
 SPLIT = 32
 TILE = 512
 UNIT = 256
-RING = 32
-CREDIT = 16
+RING = 16
+CREDIT = 8
 RIGHTS = 4
-EARLY = ({1: 5}, {})
-LATE = ({1: 4, 3: 4}, {1: 2})
+EARLY = ({1: 3}, {})
+LATE = ({1: 2, 3: 2}, {1: 1})
 PACE = RIGHT // (2 * CHUNK)
 MESH = pl.DeviceIdType.MESH
 

time: 101 us -> 101 us (level)
  no operation moved by 1% of the time
where the time goes in v3:
time: 101 us
  Pallas kernels  101 us (100%)
    pallas_call x1, Pallas kernels, per_device(): pl.pallas_call(functools.partial(kernel, n_rows, n_cols, window), out_sha...  98.6 us
    pallas_call x1, Pallas kernels, per_device(): pl.pallas_call(finish, out_shape=jax.ShapeDtypeStruct((block_rows, block_...  2.03 us

profile of v3, /device:TPU:12, one launch (start us, length us, event | category | flops | bytes accessed | tf_op | source)
XLA Modules:
  0.0 100.7 jit_solution(10975167227263033817)
XLA Ops:
  0.0 98.6 %shard_map.17 = (bf16[2048,1024]{1,0:T(8,128)(2,1)S(1)}, bf16[2,2048,1024]{2,1,0:T(8,128)(2,1)S(1)}, bf16[2048,1024]{1,0:T(8,128)(2,1)S(1)}, f32[128,1024]{1,0:T(8,128)S(1)}) custom-call(s32[2048,1024]{1,0:T(8,128)} %adj_hbm.1), custom_call_target="tpu_custom_call" | custom-call | tf_op jit(solution)/shard_map/pallas_call | solution.py:432
  98.6 2.0 %shard_map.18 = bf16[2048,1024]{1,0:T(8,128)(2,1)} custom-call(bf16[2048,1024]{1,0:T(8,128)(2,1)S(1)} %get-tuple-element.9.closed, bf16[2,2048,1024]{2,1,0:T(8,128)(2,1)S(1)} %get-tuple-element.10.left, bf16[2048,1024]{1,0:T(8,128)(2,1)S(1)} %get-tuple-element.11.right, f32[128,1024]{1,0:T(8,128)S(1)} %get-tuple-element.12.partial), custom_call_target="tpu_custom_call" | custom-call | tf_op jit(solution)/shard_map/pallas_call | solution.py:459

commit v4 on v1

--- a/solution.py
+++ b/solution.py
@@ -25,7 +25,7 @@
 RING = 32
 CREDIT = 16
 RIGHTS = 4
-EARLY = ({1: 5}, {})
+EARLY = ({1: 4}, {})
 LATE = ({1: 4, 3: 4}, {1: 2})
 PACE = RIGHT // (2 * CHUNK)
 MESH = pl.DeviceIdType.MESH

time: 101 us -> 101 us (level)
  no operation moved by 1% of the time
where the time goes in v4:
time: 101 us
  Pallas kernels  101 us (100%)
    pallas_call x1, Pallas kernels, per_device(): pl.pallas_call(functools.partial(kernel, n_rows, n_cols, window), out_sha...  98.9 us
    pallas_call x1, Pallas kernels, per_device(): pl.pallas_call(finish, out_shape=jax.ShapeDtypeStruct((block_rows, block_...  2.03 us

profile of v4, /device:TPU:12, one launch (start us, length us, event | category | flops | bytes accessed | tf_op | source)
XLA Modules:
  0.0 100.9 jit_solution(4225059420448466827)
XLA Ops:
  0.0 98.9 %shard_map.17 = (bf16[2048,1024]{1,0:T(8,128)(2,1)S(1)}, bf16[2,2048,1024]{2,1,0:T(8,128)(2,1)S(1)}, bf16[2048,1024]{1,0:T(8,128)(2,1)S(1)}, f32[128,1024]{1,0:T(8,128)S(1)}) custom-call(s32[2048,1024]{1,0:T(8,128)} %adj_hbm.1), custom_call_target="tpu_custom_call" | custom-call | tf_op jit(solution)/shard_map/pallas_call | solution.py:432
  98.9 2.0 %shard_map.18 = bf16[2048,1024]{1,0:T(8,128)(2,1)} custom-call(bf16[2048,1024]{1,0:T(8,128)(2,1)S(1)} %get-tuple-element.9.closed, bf16[2,2048,1024]{2,1,0:T(8,128)(2,1)S(1)} %get-tuple-element.10.left, bf16[2048,1024]{1,0:T(8,128)(2,1)S(1)} %get-tuple-element.11.right, f32[128,1024]{1,0:T(8,128)S(1)} %get-tuple-element.12.partial), custom_call_target="tpu_custom_call" | custom-call | tf_op jit(solution)/shard_map/pallas_call | solution.py:459
